TPU v7x, 32 devices: a whole 2x2x4 slice. The times are simulated.
32 devices in a mesh: cell: 4 (over z), tm: 8 (over y, x, core).
Axes of the slice: x: 2, y: 2, z: 4, core: 2. Of those that a mesh axis runs over, the one named last changes fastest.
Arguments:
- solution: float32 [8192], P(('cell', 'tm')), may hold values from -6 to 6
- residual: float32 [8192], P(('cell', 'tm')), may hold values from -8 to 8
- direction: float32 [8192], P(('cell', 'tm')), may hold values from -8 to 8
- noise_var: float32 [8192], P(('cell', 'tm')), may hold values from 0.5 to 2
- footprints: bfloat16 [65536, 128], P(('cell', 'tm')), may hold values from -0.5 to 0.5
- tile_owner: int32 [65536, 1], P(('cell', 'tm')), may hold values from 0 to 31; in each aligned block of 2048 rows (0 to 2047, 2048 to 4095, ...) at most 128 rows name the same one
- tile_block: int32 [65536], P(('cell', 'tm')), may hold values from 0 to 17
- tile_step: int32 [65536], P(('cell', 'tm')), may hold values from 0 to 255
- tile_obs: int32 [65536], P(('cell', 'tm')), may hold values from 0 to 255
- cell_cov: bfloat16 [9216, 9216], P('cell'), may hold values from -2 to 7, as said below
- time_cov: bfloat16 [2048, 2048], P('tm'), may hold values from -2 to 7, as said below
Outputs:
- new_solution: float32 [8192], P(('cell', 'tm'))
- new_residual: float32 [8192], P(('cell', 'tm'))
- new_direction: float32 [8192], P(('cell', 'tm'))
Inputs may be any that keep to these rules, and one draw needn't show every extreme that they name: `tile_owner`: among the 2048 tiles of one device, no owner is named by more than 128 of them. `cell_cov`: symmetric positive definite. `time_cov`: symmetric positive definite.
All inputs are finite; a program needn't handle non-finite values.
Results may differ from a plain program's by a relative error of at most 0.0021.
Values may be sent and summed in bfloat16 or wider, within the bound.
No kernel may reach another device: no remote copies, remote signals or barrier semaphores. Data moves between devices by JAX's collectives and lax.ppermute only.
A program may use at most 128 MiB of HBM per device.

v0:
```python
import jax
import jax.numpy as jnp
from jax import lax
from jax.sharding import PartitionSpec as P


def local(
    solution,
    residual,
    direction,
    noise_var,
    footprints,
    tile_owner,
    tile_block,
    tile_step,
    tile_obs,
    cell_cov,
    time_cov,
):
    devices = lax.axis_size("cell") * lax.axis_size("tm")
    tile_count = footprints.shape[0]
    block_len = footprints.shape[1]
    cell_local = cell_cov.shape[0]
    time_local = time_cov.shape[0]
    block_local = cell_local // block_len
    obs_local = direction.shape[0]
    capacity = max(2, 2 * tile_count // devices)
    slot_total = devices * capacity
    owner_dev = tile_owner[:, 0]
    owner_hot = (owner_dev[:, None] == jnp.arange(devices, dtype=jnp.int32)[None, :]).astype(
        jnp.int32
    )
    slot_rank = jnp.sum(jnp.cumsum(owner_hot, axis=0) * owner_hot, axis=1) - 1
    slot_index = owner_dev * capacity + slot_rank
    obs_hot = (tile_obs[:, None] == jnp.arange(obs_local, dtype=jnp.int32)[None, :]).astype(
        jnp.float32
    )
    dir_tile = jnp.dot(obs_hot, direction, precision=lax.Precision.HIGHEST).astype(jnp.bfloat16)
    tile_place = tile_step * block_local + tile_block
    send_values = jnp.zeros((slot_total, block_len), jnp.bfloat16).at[slot_index].set(footprints)
    send_dir = jnp.zeros((slot_total,), jnp.bfloat16).at[slot_index].set(dir_tile)
    send_place = jnp.zeros((slot_total,), jnp.int32).at[slot_index].set(tile_place)
    got_values, got_dir, got_place = (
        lax.all_to_all(
            send_values.reshape(devices, capacity, block_len),
            ("cell", "tm"),
            split_axis=0,
            concat_axis=0,
            tiled=True,
        ),
        lax.all_to_all(
            send_dir.reshape(devices, capacity),
            ("cell", "tm"),
            split_axis=0,
            concat_axis=0,
            tiled=True,
        ),
        lax.all_to_all(
            send_place.reshape(devices, capacity),
            ("cell", "tm"),
            split_axis=0,
            concat_axis=0,
            tiled=True,
        ),
    )
    got_values = got_values.reshape(slot_total, block_len).astype(jnp.float32)
    got_dir = got_dir.reshape(slot_total).astype(jnp.float32)
    got_place = got_place.reshape(slot_total)
    flux_time = jnp.zeros((time_local * block_local, block_len), jnp.float32)
    flux_time = flux_time.at[got_place].add(got_dir[:, None] * got_values)
    flux_grid = flux_time.reshape(time_local, cell_local).T.astype(jnp.bfloat16)
    mixed_cells = jnp.dot(
        cell_cov,
        lax.all_gather(flux_grid, "cell", axis=0, tiled=True),
        preferred_element_type=jnp.float32,
    ).astype(jnp.bfloat16)
    smoothed = lax.dot_general(
        time_cov,
        lax.all_gather(mixed_cells, "tm", axis=1, tiled=True),
        (((1,), (1,)), ((), ())),
        preferred_element_type=jnp.float32,
    )
    smoothed = smoothed.astype(jnp.bfloat16).reshape(time_local * block_local, block_len)
    slot_dots = jnp.sum(got_values * smoothed[got_place].astype(jnp.float32), axis=1)
    returned = lax.all_to_all(
        slot_dots.reshape(devices, capacity),
        ("cell", "tm"),
        split_axis=0,
        concat_axis=0,
        tiled=True,
    )
    tile_dots = returned.reshape(slot_total)[slot_index]
    applied = jnp.dot(tile_dots, obs_hot, precision=lax.Precision.HIGHEST) + noise_var * direction
    norm_now = lax.psum(jnp.sum(residual * residual), ("cell", "tm"))
    curvature = lax.psum(jnp.sum(direction * applied), ("cell", "tm"))
    step_size = norm_now / curvature
    new_solution = solution + step_size * direction
    new_residual = residual - step_size * applied
    norm_next = lax.psum(jnp.sum(new_residual * new_residual), ("cell", "tm"))
    new_direction = new_residual + norm_next / norm_now * direction
    return (new_solution, new_residual, new_direction)


def solution(mesh):
    return jax.shard_map(
        local,
        mesh=mesh,
        in_specs=(
            P(("cell", "tm")),
            P(("cell", "tm")),
            P(("cell", "tm")),
            P(("cell", "tm")),
            P(("cell", "tm"), None),
            P(("cell", "tm"), None),
            P(("cell", "tm")),
            P(("cell", "tm")),
            P(("cell", "tm")),
            P("cell", None),
            P("tm", None),
        ),
        out_specs=(P(("cell", "tm")), P(("cell", "tm")), P(("cell", "tm"))),
        check_vma=False,
    )
```

profile of v0, /device:TPU:0, one launch (start us, length us, event | category | flops | bytes accessed | tf_op | source)
XLA Modules:
  0.0 438.2 jit_solution(13048471341326374734)
XLA Ops:
  7.2 1.8 fusion.4
  9.0 0.7 fusion.13
  9.8 9.1 %reduce-window.6 = s32[32,16,128]{2,1,0:T(8,128)S(1)} reduce-window(s32[32,16,128]{2,1,0:T(8,128)S(1)} %fusion.13, s32[]{:T(128)} %constant.11.clone.1), window={size=1x1x128 pad=0_0x0_0x127_0}, to_apply=%region_2.3 | reduce-window | flops 8323072 | bytes 524292 | tf_op jit(solution)/shard_map/reduce-window
  19.7 14.6 %scatter_custom_fusion.2 = bf16[4096]{0:T(1024)(128)(2,1)S(1)} fusion(s32[2048]{0:T(1024)S(1)} %bitcast.62, bf16[2048]{0:T(1024)(128)(2,1)S(1)} %convert_element_type.58, bf16[]{:T(256)} %constant.9.clone.1), kind=kCustom, calls=%fused_computation.36 | custom fusion | bytes 8194 | tf_op jit(solution)/shard_map/scatter | solution.py:41
  34.3 0.6 copy.19
  34.9 7.3 %all-to-all-start.2 = ((bf16[32,1,128]{2,1,0:T(2,128)(2,1)}), bf16[32,1,128]{2,1,0:T(2,128)(2,1)S(1)}, u32[]{:S(2)}, u32[]{:S(2)}) async-start(bf16[32,1,128]{2,1,0:T(2,128)(2,1)} %copy.19), calls=%async_computation.2 | async-start | bytes 32768 | tf_op jit(solution)/shard_map/all_to_all | solution.py:51
  42.3 8.6 %scatter_custom_fusion.1 = s32[4096]{0:T(1024)} fusion(s32[2048]{0:T(1024)S(1)} %bitcast.63, s32[2048]{0:T(1024)S(1)} %multiply_add_fusion, s32[]{:T(128)} %constant.11.clone.1), kind=kCustom, calls=%fused_computation.33 | custom fusion | bytes 16388 | tf_op jit(solution)/shard_map/scatter | solution.py:42
  50.9 5.8 %all-to-all-start.1 = ((s32[32,1,128]{2,1,0:T(1,128)}), s32[32,1,128]{2,1,0:T(1,128)S(1)}, u32[]{:S(2)}, u32[]{:S(2)}) async-start(s32[32,1,128]{2,1,0:T(1,128)} %bitcast.8), calls=%async_computation.1 | async-start | bytes 32768 | tf_op jit(solution)/shard_map/all_to_all | solution.py:58
  56.8 7.2 %scatter_custom_fusion = bf16[4096,128]{1,0:T(8,128)(2,1)} fusion(s32[2048]{0:T(1024)S(1)} %bitcast.64, bf16[2048,128]{1,0:T(8,128)(2,1)} %param.15, bf16[]{:T(256)} %constant.9.clone.1), kind=kCustom, calls=%fused_computation.20 | custom fusion | bytes 1049088 | tf_op jit(solution)/shard_map/scatter | solution.py:40
  63.9 5.8 %all-to-all-start = ((bf16[32,128,128]{2,1,0:T(8,128)(2,1)}), bf16[32,128,128]{2,1,0:T(8,128)(2,1)S(1)}, u32[]{:S(2)}, u32[]{:S(2)}) async-start(bf16[32,128,128]{2,1,0:T(8,128)(2,1)} %bitcast.7), calls=%async_computation | async-start | bytes 2097152 | tf_op jit(solution)/shard_map/all_to_all | solution.py:44
  69.9 26.1 %all-to-all-done = bf16[32,128,128]{2,1,0:T(8,128)(2,1)S(1)} async-done(((bf16[32,128,128]{2,1,0:T(8,128)(2,1)}), bf16[32,128,128]{2,1,0:T(8,128)(2,1)S(1)}, u32[]{:S(2)}, u32[]{:S(2)}) %all-to-all-start) | async-done | bytes 1048608 | tf_op jit(solution)/shard_map/all_to_all | solution.py:44
  96.0 1.9 bitcast_multiply_fusion
  97.9 28.3 %scatter_custom_fusion.3 = f32[4608,128]{1,0:T(8,128)} fusion(s32[4096]{0:T(1024)S(1)} %bitcast.60, f32[4096,128]{1,0:T(8,128)} %bitcast_multiply_fusion, f32[]{:T(128)} %constant.8.clone.1), kind=kCustom, calls=%fused_computation.16 | custom fusion | flops 524288 | bytes 2359808 | tf_op jit(solution)/shard_map/scatter-add | solution.py:70
  126.2 1.8 convert_element_type.63
  128.0 2.2 convert_element_type.64
  130.2 88.7 %all-gather.3.cloned.1.call-done = bf16[9216,256]{0,1:T(8,128)(2,1)} async-done(((bf16[2304,256]{0,1:T(8,128)(2,1)}), bf16[9216,256]{0,1:T(8,128)(2,1)}) %all-gather.3.cloned.1.call-update) | async-done | bytes 4718608 | tf_op jit(solution)/shard_map/all_gather | solution.py:74
  218.9 19.5 %fusion.1 = bf16[2304,256]{0,1:T(8,128)(2,1)} fusion(bf16[9216,256]{0,1:T(8,128)(2,1)} %all-gather.3.cloned.1.call-done, bf16[2304,9216]{1,0:T(8,128)(2,1)} %param.20), kind=kOutput, calls=%fused_computation.9 | convolution fusion | flops 10872225792 | bytes 48365568 | tf_op jit(solution)/shard_map/dot_general | solution.py:72
  238.4 57.3 %all-gather.5.cloned.1.call-done = bf16[2304,2048]{0,1:T(8,128)(2,1)} async-done(((bf16[2304,256]{0,1:T(8,128)(2,1)}), bf16[2304,2048]{0,1:T(8,128)(2,1)}) %all-gather.5.cloned.1.call-update) | async-done | bytes 9437200 | tf_op jit(solution)/shard_map/all_gather | solution.py:79
  295.7 6.3 %fusion = bf16[256,2304]{0,1:T(8,128)(2,1)S(1)} fusion(bf16[2304,2048]{0,1:T(8,128)(2,1)} %all-gather.5.cloned.1.call-done, bf16[256,2048]{1,0:T(8,128)(2,1)S(1)} %copy-done), kind=kOutput, calls=%fused_computation.8 | convolution fusion | flops 2416508928 | bytes 11665408 | tf_op jit(solution)/shard_map/dot_general | solution.py:77
  302.0 1.5 copy.20
  303.5 2.7 reshape.108
  306.3 14.9 %gather_fusion = bf16[4096,128]{1,0:T(8,128)(2,1)} fusion(bf16[4608,128]{1,0:T(8,128)(2,1)S(1)} %reshape.108, s32[4096]{0:T(1024)S(1)} %broadcast_clamp_fusion), kind=kCustom, calls=%fused_computation | custom fusion | bytes 2113536 | tf_op jit(solution)/shard_map/gather | solution.py:84
  321.2 2.4 fusion.2
  323.6 4.6 %all-to-all-start.3 = ((f32[32,1,128]{2,1,0:T(1,128)}), f32[32,1,128]{2,1,0:T(1,128)S(1)}, u32[]{:S(2)}, u32[]{:S(2)}) async-start(f32[32,1,128]{2,1,0:T(1,128)} %bitcast.20), calls=%async_computation.3 | async-start | bytes 32768 | tf_op jit(solution)/shard_map/all_to_all | solution.py:85
  328.2 7.2 %all-to-all-done.3 = f32[32,1,128]{2,1,0:T(1,128)S(1)} async-done(((f32[32,1,128]{2,1,0:T(1,128)}), f32[32,1,128]{2,1,0:T(1,128)S(1)}, u32[]{:S(2)}, u32[]{:S(2)}) %all-to-all-start.3) | async-done | bytes 16416 | tf_op jit(solution)/shard_map/all_to_all | solution.py:85
  335.4 11.8 %gather_fusion.1 = f32[2048]{0:T(1024)S(1)} fusion(f32[4096]{0:T(1024)S(1)} %bitcast.51, s32[2048]{0:T(1024)S(1)} %broadcast_clamp_fusion.1), kind=kCustom, calls=%fused_computation.1 | custom fusion | bytes 24576 | tf_op jit(solution)/shard_map/gather | solution.py:92
  347.2 0.8 fusion.3
  348.0 0.6 multiply_reduce_fusion.1
  348.6 38.5 %all-reduce = (f32[]{:T(128)}, f32[]{:T(128)}) all-reduce(f32[]{:T(128)} %get-tuple-element.10, f32[]{:T(128)} %get-tuple-element.9), channel_id=1, replica_groups=mesh['cell'=4,'tm'=8] {'cell','tm'}, use_global_device_ids=true, to_apply=%region_1.2 | all-reduce | flops 2 | bytes 16 | tf_op jit(solution)/shard_map/psum | solution.py:94
  388.5 0.6 multiply_reduce_fusion
  389.1 40.4 %psum.23 = f32[]{:T(128)} all-reduce(f32[]{:T(128)} %get-tuple-element.5), channel_id=1, replica_groups=mesh['cell'=4,'tm'=8] {'cell','tm'}, use_global_device_ids=true, to_apply=%region_13.14 | all-reduce | flops 1 | bytes 8 | tf_op jit(solution)/shard_map/psum | solution.py:99
  430.8 0.6 multiply_add_fusion.1
  (39 shorter events, 1.1 us)
Async XLA Ops:
  7.2 288.5 %copy-start = (bf16[256,2048]{1,0:T(8,128)(2,1)S(1)}, bf16[256,2048]{1,0:T(8,128)(2,1)}, u32[]{:S(2)}) copy-start(bf16[256,2048]{1,0:T(8,128)(2,1)} %param.21) | copy-start | bytes 3145732
  7.2 12.4 %copy-start.1 = (s32[2048,1]{0,1:T(1,128)S(1)}, s32[2048,1]{0,1:T(1,128)}, u32[]{:S(2)}) copy-start(s32[2048,1]{0,1:T(1,128)} %param.16) | copy-start | bytes 24580
  7.2 35.1 %copy-start.4 = (s32[2048]{0:T(1024)S(1)}, s32[2048]{0:T(1024)}, u32[]{:S(2)}) copy-start(s32[2048]{0:T(1024)} %param.18) | copy-start | bytes 24580
  7.2 35.1 %copy-start.3 = (s32[2048]{0:T(1024)S(1)}, s32[2048]{0:T(1024)}, u32[]{:S(2)}) copy-start(s32[2048]{0:T(1024)} %param.17) | copy-start | bytes 24580
  34.9 16.0 %all-to-all-start.2 = ((bf16[32,1,128]{2,1,0:T(2,128)(2,1)}), bf16[32,1,128]{2,1,0:T(2,128)(2,1)S(1)}, u32[]{:S(2)}, u32[]{:S(2)}) async-start(bf16[32,1,128]{2,1,0:T(2,128)(2,1)} %copy.19), calls=%async_computation.2 | async-start | bytes 32768 | tf_op jit(solution)/shard_map/all_to_all | solution.py:51
  50.9 13.0 %all-to-all-start.1 = ((s32[32,1,128]{2,1,0:T(1,128)}), s32[32,1,128]{2,1,0:T(1,128)S(1)}, u32[]{:S(2)}, u32[]{:S(2)}) async-start(s32[32,1,128]{2,1,0:T(1,128)} %bitcast.8), calls=%async_computation.1 | async-start | bytes 32768 | tf_op jit(solution)/shard_map/all_to_all | solution.py:58
  63.9 32.0 %all-to-all-start = ((bf16[32,128,128]{2,1,0:T(8,128)(2,1)}), bf16[32,128,128]{2,1,0:T(8,128)(2,1)S(1)}, u32[]{:S(2)}, u32[]{:S(2)}) async-start(bf16[32,128,128]{2,1,0:T(8,128)(2,1)} %bitcast.7), calls=%async_computation | async-start | bytes 2097152 | tf_op jit(solution)/shard_map/all_to_all | solution.py:44
  69.8 149.1 %all-gather.3.cloned.1.call-start = ((), (), s32[]{:S(2)}) async-start(), calls=%async_computation.4 | async-start | bytes 5898240 | tf_op jit(solution)/shard_map/all_gather | solution.py:74
  130.2 165.5 %all-gather.5.cloned.1.call-start = ((), (), s32[]{:S(2)}) async-start(), calls=%async_computation.5 | async-start | bytes 10616832 | tf_op jit(solution)/shard_map/all_gather | solution.py:79
  323.6 11.8 %all-to-all-start.3 = ((f32[32,1,128]{2,1,0:T(1,128)}), f32[32,1,128]{2,1,0:T(1,128)S(1)}, u32[]{:S(2)}, u32[]{:S(2)}) async-start(f32[32,1,128]{2,1,0:T(1,128)} %bitcast.20), calls=%async_computation.3 | async-start | bytes 32768 | tf_op jit(solution)/shard_map/all_to_all | solution.py:85
  335.4 11.8 %copy-start.9 = (s32[2048]{0:T(1024)S(1)}, s32[2048]{0:T(1024)}, u32[]{:S(2)}) copy-start(s32[2048]{0:T(1024)} %param.19) | copy-start | bytes 24580
  335.4 12.6 %copy-start.2 = (f32[256]{0:T(256)S(1)}, f32[256]{0:T(256)}, u32[]{:S(2)}) copy-start(f32[256]{0:T(256)} %param.13) | copy-start | bytes 3076
  335.4 12.6 %copy-start.5 = (f32[256]{0:T(256)S(1)}, f32[256]{0:T(256)}, u32[]{:S(2)}) copy-start(f32[256]{0:T(256)} %param.12) | copy-start | bytes 3076
  335.4 12.6 %copy-start.6 = (f32[256]{0:T(256)S(1)}, f32[256]{0:T(256)}, u32[]{:S(2)}) copy-start(f32[256]{0:T(256)} %param.14) | copy-start | bytes 3076
  335.4 95.4 %copy-start.8 = (f32[256]{0:T(256)S(1)}, f32[256]{0:T(256)}, u32[]{:S(2)}) copy-start(f32[256]{0:T(256)} %param.11) | copy-start | bytes 3076
  389.1 42.3 %copy-start.7 = (f32[256]{0:T(256)}, f32[256]{0:T(256)S(1)}, u32[]{:S(2)}) copy-start(f32[256]{0:T(256)S(1)} %get-tuple-element.6) | copy-start | bytes 3076
Sparse Core Ops, SparseCore 0:
  130.3 88.5 all-gather.2
  238.5 57.0 all-gather.4
where the time goes:
time: 438 us
  waiting for transfers between devices  179 us (41%)
  blocking collectives  78.8 us (18%)
  local copies, waits for them, and re-layouts  64.5 us (15%)
  other arithmetic  46.5 us (11%)
  matrix products  28.4 us (6%)
  starting transfers between devices  23.7 us (5%)
  between operations  17 us (4%)
    all_gather x1, waiting for transfers between devices, local(): lax.all_gather(flux_grid, 'cell', axis=0, tiled=True)  88.7 us
    all_gather x1, waiting for transfers between devices, local(): lax.all_gather(mixed_cells, 'tm', axis=1, tiled=True)  57.3 us
    psum x1, blocking collectives, local(): norm_next = lax.psum(jnp.sum(new_residual * new_residual), ('cell', 'tm'))  40.4 us
    psum x1, blocking collectives, local(): norm_now = lax.psum(jnp.sum(residual * residual), ('cell', 'tm'))  38.5 us
    scatter-add x1, other arithmetic, local(): flux_time = flux_time.at[got_place].add(got_dir[:, None] * got_values)  28.3 us
    all_to_all x1, waiting for transfers between devices, local(): lax.all_to_all(send_values.reshape(devices, capacity, block_len), ('cell'...  26.1 us
    dot_general x1, matrix products, local(): jnp.dot(cell_cov, lax.all_gather(flux_grid, 'cell', axis=0, tiled=True),...  19.5 us
    gather x1, local copies, waits for them, and re-layouts, local(): smoothed[got_place].astype(jnp.float32)  14.9 us
  transfers between devices with their start and end apart: 6, of which 4 were waited for; matrix products, arithmetic and copies ran while one was open for 4% of the time, Pallas kernels for 0%

commit v1 on v0

v1 whole, which is shorter than its diff:
```python
import functools

import jax
import jax.numpy as jnp
from jax import lax
from jax.experimental import pallas as pl
from jax.experimental.pallas import tpu as pltpu
from jax.sharding import PartitionSpec as P

AXES = ("cell", "tm")
LANES = 128
META = 16
UNROLL = 8
COPIES = 4
F32 = jnp.float32
BF16 = jnp.bfloat16
VMEM = pl.BlockSpec(memory_space=pltpu.VMEM)
SMEM = pl.BlockSpec(memory_space=pltpu.SMEM)


def pack_kernel(devices, cap, owner, step, block, obs, dir_col, tiles, send, slot_obs, rhs):
    rows = owner.shape[0]
    obs_local = dir_col.shape[0]
    width = tiles.shape[1]
    groups = devices * cap // LANES
    lane_i = lax.broadcasted_iota(jnp.int32, (LANES, 2 * LANES), 0)
    lane_j = lax.broadcasted_iota(jnp.int32, (LANES, 2 * LANES), 1)
    tri = jnp.where((lane_i <= lane_j) | (lane_j >= LANES), 1.0, 0.0).astype(BF16)
    dev_i = lax.broadcasted_iota(jnp.int32, (devices, LANES), 0)
    obs_i = lax.broadcasted_iota(jnp.int32, (obs_local, LANES), 0)
    eight = lax.broadcasted_iota(jnp.int32, (8, LANES), 0)
    directions = jnp.broadcast_to(dir_col[...], (obs_local, LANES))
    rhs[:, :width] = tiles[...]
    carry = jnp.zeros((devices, LANES), F32)
    slots = []
    for r in range(rows):
        own = owner[r : r + 1, :]
        hot = jnp.where(dev_i == own, 1.0, 0.0)
        counts = jnp.dot(hot.astype(BF16), tri, preferred_element_type=F32)
        rank = jnp.sum(hot * (counts[:, :LANES] + carry), axis=0, keepdims=True)
        carry = carry + counts[:, LANES:]
        slots.append(own * cap + rank.astype(jnp.int32) - 1)
        seen = obs[r : r + 1, :]
        d = jnp.sum(jnp.where(obs_i == seen, directions, 0.0), axis=0, keepdims=True)
        hi = d.astype(BF16).astype(F32)
        mid = (d - hi).astype(BF16).astype(F32)
        low = d - hi - mid
        meta = jnp.zeros((8, LANES), F32)
        fields = (hi, mid, low, step[r : r + 1, :].astype(F32), block[r : r + 1, :].astype(F32), seen.astype(F32) + 1.0)
        for f, value in enumerate(fields):
            meta = jnp.where(eight == f, value, meta)
        full = jnp.concatenate([meta, jnp.zeros((LANES - 8, LANES), F32)], axis=0)
        rhs[r * LANES : (r + 1) * LANES, width:] = full.T.astype(BF16)
    slot_i = lax.broadcasted_iota(jnp.int32, (LANES, LANES), 0)
    share = LANES // cap

    def group(g, _):
        base = slot_i + g * LANES
        pick = jnp.concatenate([jnp.where(base == s, 1.0, 0.0).astype(BF16) for s in slots], axis=1)
        out = jnp.dot(pick, rhs[...], preferred_element_type=F32)
        meta = out[:, width:].T
        for q in range(share):
            send[g * share + q, :cap, :] = out[q * cap : (q + 1) * cap, :width].astype(BF16)
            part = meta[:META, :]
            if q:
                part = jnp.concatenate([part[:, q * cap :], part[:, : q * cap]], axis=1)
            send[g * share + q, cap:, :] = part.astype(BF16)
        slot_obs[pl.ds(g, 1), :] = meta[5:6, :]
        return 0

    lax.fori_loop(0, groups, group, 0)


def scatter_kernel(devices, cap, sizes, time_local, place, weight, count, got, *refs):
    outs, (values, *sums) = refs[: len(sizes)], refs[len(sizes) :]
    for s in sums:
        s[...] = jnp.zeros_like(s)

    def widen(s, _):
        values[pl.ds(s * cap, cap), :] = got[s, :cap, :].astype(F32)
        return 0

    lax.fori_loop(0, devices, widen, 0)

    def source(s, _):
        def some(k, _):
            base = s * cap + k * UNROLL
            for u in range(UNROLL):
                at = place[base + u]
                acc = sums[u % COPIES]
                acc[pl.ds(at, 1), :] += values[pl.ds(base + u, 1), :] * weight[base + u]
            return 0

        return lax.fori_loop(0, pl.cdiv(count[s], UNROLL), some, 0)

    lax.fori_loop(0, devices, source, 0)
    first = 0
    for out, size in zip(outs, sizes):
        for b in range(size):
            rows = slice((first + b) * time_local, (first + b + 1) * time_local)
            total = sums[0][rows, :]
            for s in sums[1:]:
                total = total + s[rows, :]
            out[:, b * LANES : (b + 1) * LANES] = total.astype(BF16)
        first += size


def gather_kernel(devices, cap, block_local, time_local, place, count, got, smoothed, dirs, residual, direction, noise, ret, flat, picked):
    for b in range(block_local):
        part = smoothed[b * LANES : (b + 1) * LANES, :].T
        flat[b * time_local : (b + 1) * time_local, :] = part.astype(BF16).astype(F32)
    picked[...] = jnp.zeros_like(picked)

    def source(s, _):
        def some(k, _):
            base = s * cap + k * UNROLL
            for u in range(UNROLL):
                picked[pl.ds(base + u, 1), :] = flat[pl.ds(place[base + u], 1), :]
            return 0

        return lax.fori_loop(0, pl.cdiv(count[s], UNROLL), some, 0)

    lax.fori_loop(0, devices, source, 0)
    share = LANES // cap

    def dots(g, total):
        tiles = [got[g * share + q, :cap, :].astype(F32) for q in range(share)]
        tiles = tiles[0] if share == 1 else jnp.concatenate(tiles, axis=0)
        prod = tiles * picked[pl.ds(g * LANES, LANES), :]
        row = jnp.sum(prod.T, axis=0, keepdims=True)
        for q in range(share):
            part = row
            if q:
                part = jnp.concatenate([row[:, q * cap :], row[:, : q * cap]], axis=1)
            ret[g * share + q, 0:1, :] = part
        return total + row * dirs[pl.ds(g, 1), :]

    total = lax.fori_loop(0, devices // share, dots, jnp.zeros((1, LANES), F32))
    d = direction[...]
    curv = jnp.sum(total) + jnp.sum(noise[...] * d * d)
    norm = jnp.sum(residual[...] * residual[...])
    lane = lax.broadcasted_iota(jnp.int32, (1, LANES), 1)
    scalars = jnp.where(lane == 0, curv, jnp.where(lane == 1, norm, 0.0))

    def spread(s, _):
        ret[s, 1:2, :] = scalars
        return 0

    lax.fori_loop(0, devices, spread, 0)


def finish_kernel(devices, dots, scalars, slot_obs, solution, residual, direction, noise, new_solution, new_residual, share, ratio):
    rows = slot_obs.shape[0]
    blocks = solution.shape[0]
    obs_local = blocks * LANES
    obs_i = lax.broadcasted_iota(jnp.int32, (obs_local, LANES), 0).astype(F32) + 1.0
    acc = jnp.zeros((obs_local, LANES), F32)
    for r in range(rows):
        acc = acc + jnp.where(obs_i == slot_obs[r : r + 1, :], dots[r : r + 1, :], 0.0)
    parts = [jnp.sum(acc[b * LANES : (b + 1) * LANES, :].T, axis=0, keepdims=True) for b in range(blocks)]
    d = direction[...]
    applied = jnp.concatenate(parts, axis=0) + noise[...] * d
    sums = jnp.sum(scalars[...], axis=0, keepdims=True)
    lane = lax.broadcasted_iota(jnp.int32, (1, LANES), 1)
    curvature = jnp.sum(jnp.where(lane == 0, sums, 0.0), keepdims=True)
    norm_now = jnp.sum(jnp.where(lane == 1, sums, 0.0), keepdims=True)
    step = norm_now / curvature
    new_solution[...] = solution[...] + step * d
    fresh = residual[...] - step * applied
    new_residual[...] = fresh
    share[...] = jnp.broadcast_to(jnp.sum(fresh * fresh, keepdims=True).reshape(1, 1, 1), share.shape)
    ratio[...] = jnp.broadcast_to(norm_now, ratio.shape)


def product_kernel(step, sizes, planes, here, *refs):
    flux, cov, refs = refs[: -2 - (step > 0)], refs[-2 - (step > 0)], refs[-1 - (step > 0) :]
    out = refs[-1]
    q = pl.program_id(1)

    if step:

        @pl.when(q == 0)
        def _():
            out[...] = refs[0][...]

    for side in range(len(flux) // len(sizes)):
        plane = meets(step, side, here[0])

        @pl.when((q == side) & (plane >= 0) & (plane < planes))
        def _(side=side):
            total, at = None, 0
            for k, size in enumerate(sizes):
                part = jnp.dot(cov[:, at : at + size], flux[side * len(sizes) + k][...], preferred_element_type=F32)
                total = part if total is None else total + part
                at += size
            out[...] = out[...] + total if step else total


def meets(step, side, here):
    return here + step if side else here - step


def product(step, sides, cell_cov, acc, planes, here):
    flux = [x for side in sides for x in side]
    sizes = [x.shape[0] for x in sides[0]]
    width, steps = sum(sizes), flux[0].shape[1]
    out = cell_cov.shape[0]
    tile = next(t for t in (384, 256, 128) if out % t == 0)
    keep = pl.BlockSpec((tile, steps), lambda i, q, h: (i, 0))

    def column(i, q, h):
        left = h[0] - step
        right = h[0] + step
        first = jnp.where(left >= 0, left, jnp.minimum(right, planes - 1))
        second = jnp.where(right < planes, right, jnp.maximum(left, 0))
        return i, jnp.where(q == 0, first, second)

    return pl.pallas_call(
        functools.partial(product_kernel, step, sizes, planes),
        grid_spec=pltpu.PrefetchScalarGridSpec(
            num_scalar_prefetch=1,
            grid=(out // tile, len(sides)),
            in_specs=[pl.BlockSpec(x.shape, lambda i, q, h: (0, 0)) for x in flux]
            + [pl.BlockSpec((tile, width), column)] + ([keep] if step else []),
            out_specs=keep,
        ),
        out_shape=jax.ShapeDtypeStruct((out, steps), F32),
        cost_estimate=pl.CostEstimate(flops=2 * steps * width * out, bytes_accessed=2 * out * width, transcendentals=0),
        name="product",
    )(here, *flux, cell_cov, *([acc] if step else []))


def shift(x, by):
    n = lax.axis_size("cell")
    return lax.ppermute(x, "cell", [(i, i + by) for i in range(n) if 0 <= i + by < n])


def smooth(flux, cell_cov, time_cov):
    n = lax.axis_size("cell")
    here = lax.axis_index("cell").astype(jnp.int32).reshape(1)
    mixed = []
    for f in flux:
        whole = lax.all_gather(f, "tm", axis=0, tiled=True)
        part = lax.dot_general(whole, time_cov, (((0,), (1,)), ((), ())), preferred_element_type=F32)
        mixed.append(part.astype(BF16))
    right, left = mixed, mixed
    total = product(0, [mixed], cell_cov, None, n, here)
    for s in range(1, n):
        right = [shift(x, 1) for x in right]
        left = [shift(x, -1) for x in left]
        total = product(s, [right, left], cell_cov, total, n, here)
    return total


def local(solution, residual, direction, noise_var, footprints, tile_owner, tile_block, tile_step, tile_obs, cell_cov, time_cov):
    devices = lax.axis_size("cell") * lax.axis_size("tm")
    tile_count, block_len = footprints.shape
    cell_local = cell_cov.shape[0]
    time_local = time_cov.shape[0]
    block_local = cell_local // block_len
    obs_local = direction.shape[0]
    cap = max(2, 2 * tile_count // devices)
    slots = devices * cap
    assert block_len == LANES and LANES % cap == 0 and cap % UNROLL == 0
    assert max(time_local, block_local, obs_local) <= 256
    half = (block_local + 1) // 2
    sizes = (half, block_local - half)
    rows = (tile_count // LANES, LANES)
    send, slot_obs = pl.pallas_call(
        functools.partial(pack_kernel, devices, cap),
        out_shape=(
            jax.ShapeDtypeStruct((devices, cap + META, LANES), BF16),
            jax.ShapeDtypeStruct((slots // LANES, LANES), F32),
        ),
        in_specs=[VMEM] * 6,
        out_specs=(VMEM, VMEM),
        scratch_shapes=[pltpu.VMEM((tile_count, 2 * LANES), BF16)],
        name="pack",
    )(
        tile_owner.reshape(rows),
        tile_step.reshape(rows),
        tile_block.reshape(rows),
        tile_obs.reshape(rows),
        direction.reshape(obs_local, 1),
        footprints,
    )
    got = lax.all_to_all(send, AXES, split_axis=0, concat_axis=0, tiled=True)
    meta = got[:, cap : cap + 6, :cap].astype(F32)
    place = (meta[:, 4] * time_local + meta[:, 3]).astype(jnp.int32).reshape(slots)
    weight = meta[:, 0].reshape(slots)
    dirs = (meta[:, 0] + meta[:, 1] + meta[:, 2]).reshape(slots // LANES, LANES)
    count = jnp.sum((meta[:, 5] > 0).astype(jnp.int32), axis=1)
    flat = pltpu.VMEM((block_local * time_local, LANES), F32)
    flux = pl.pallas_call(
        functools.partial(scatter_kernel, devices, cap, sizes, time_local),
        out_shape=[jax.ShapeDtypeStruct((time_local, size * LANES), BF16) for size in sizes],
        in_specs=[SMEM] * 3 + [VMEM],
        out_specs=[VMEM] * len(sizes),
        scratch_shapes=[pltpu.VMEM((slots, LANES), F32)] + [flat] * COPIES,
        name="scatter",
    )(place, weight, count, got)
    smoothed = smooth(flux, cell_cov, time_cov)
    wide = (obs_local // LANES, LANES)
    solution, residual, direction, noise_var = (x.reshape(wide) for x in (solution, residual, direction, noise_var))
    ret = pl.pallas_call(
        functools.partial(gather_kernel, devices, cap, block_local, time_local),
        out_shape=jax.ShapeDtypeStruct((devices, 2, LANES), F32),
        in_specs=[SMEM] * 2 + [VMEM] * 6,
        out_specs=VMEM,
        scratch_shapes=[flat, pltpu.VMEM((slots, LANES), F32)],
        name="gather",
    )(place, count, got, smoothed, dirs, residual, direction, noise_var)
    back = lax.all_to_all(ret, AXES, split_axis=0, concat_axis=0, tiled=True)
    new_solution, new_residual, share, norm_now = pl.pallas_call(
        functools.partial(finish_kernel, devices),
        out_shape=(
            jax.ShapeDtypeStruct(wide, F32),
            jax.ShapeDtypeStruct(wide, F32),
            jax.ShapeDtypeStruct((devices, 1, LANES), F32),
            jax.ShapeDtypeStruct((1, LANES), F32),
        ),
        in_specs=[VMEM] * 7,
        out_specs=(VMEM,) * 4,
        name="finish",
    )(back[:, 0, :cap].reshape(slots // LANES, LANES), back[:, 1, :], slot_obs, solution, residual, direction, noise_var)
    shares = lax.all_to_all(share, AXES, split_axis=0, concat_axis=0, tiled=True)
    norm_next = jnp.sum(shares[:, 0, 0])
    new_direction = new_residual + norm_next / norm_now[0, 0] * direction
    return tuple(x.reshape(obs_local) for x in (new_solution, new_residual, new_direction))


def solution(mesh):
    shared = P(AXES)
    return jax.shard_map(
        local,
        mesh=mesh,
        in_specs=(shared,) * 4 + (P(AXES, None), P(AXES, None)) + (shared,) * 3 + (P("cell", None), P("tm", None)),
        out_specs=(shared,) * 3,
        check_vma=False,
    )
```

time: 438 us -> 321 us (0.73)
  Pallas kernels: 0 us -> 85.6 us
  waiting for transfers between devices: 179 us -> 98.6 us
  local copies, waits for them, and re-layouts: 64.5 us -> 2.24 us
  other arithmetic: 46.5 us -> 3.21 us
  matrix products: 28.4 us -> 7.56 us
  starting transfers between devices: 23.7 us -> 35.7 us
  blocking collectives: 78.8 us -> 71.7 us
    pallas_call x0 -> x8, Pallas kernels: none -> 85.6 us  [the longest x4 44.5 us: product(): pl.pallas_call(functools.partial(product_kernel, step, sizes, planes), gr...]
    psum x2 -> x0, blocking collectives: 78.8 us -> none  [the longest x1 40.4 us: local(): norm_next = lax.psum(jnp.sum(new_residual * new_residual), ('cell', 'tm'))]
    all_gather x2, waiting for transfers between devices: 146 us -> 70.7 us  [smooth(): whole = lax.all_gather(f, 'tm', axis=0, tiled=True)]
    all_to_all x0 -> x3, blocking collectives: none -> 71.7 us  [the longest x1 38 us: local(): got = lax.all_to_all(send, AXES, split_axis=0, concat_axis=0, tiled=True)]
    ppermute x0 -> x12, starting transfers between devices: none -> 35.6 us  [shift(): lax.ppermute(x, 'cell', [(i, i + by) for i in range(n) if 0 <= i + by < n])]
    all_to_all x4 -> x0, waiting for transfers between devices: 33.3 us -> none  [the longest x1 26.1 us: local(): lax.all_to_all(send_values.reshape(devices, capacity, block_len), ('cell'...]
    scatter x3 -> x0, local copies, waits for them, and re-layouts: 30.4 us -> none  [the longest x1 14.6 us: local(): jnp.zeros((slot_total,), jnp.bfloat16).at[slot_index].set(dir_tile)]
    scatter-add x1 -> x0, other arithmetic: 28.3 us -> none  [local(): flux_time = flux_time.at[got_place].add(got_dir[:, None] * got_values)]
  transfers between devices with their start and end apart: 6 -> 14, of which waited for: 4 -> 7; matrix products, arithmetic and copies ran while one was open for 4% -> 2% of each run, Pallas kernels for 0% -> 10%
where the time goes in v1:
time: 321 us; the launch traced here: 320 us
  waiting for transfers between devices  98.6 us (31%)
  Pallas kernels  85.6 us (27%)
  blocking collectives  71.7 us (22%)
  starting transfers between devices  35.7 us (11%)
  between operations  15.5 us (5%)
  matrix products  7.56 us (2%)
  other arithmetic  3.21 us (1%)
    all_gather x2, waiting for transfers between devices, smooth(): whole = lax.all_gather(f, 'tm', axis=0, tiled=True)  70.7 us
    pallas_call x4, Pallas kernels, product(): pl.pallas_call(functools.partial(product_kernel, step, sizes, planes), gr...  44.5 us
    all_to_all x1, blocking collectives, local(): got = lax.all_to_all(send, AXES, split_axis=0, concat_axis=0, tiled=True)  38 us
    ppermute x12, starting transfers between devices, shift(): lax.ppermute(x, 'cell', [(i, i + by) for i in range(n) if 0 <= i + by < n])  35.6 us
    ppermute x12, waiting for transfers between devices, shift(): lax.ppermute(x, 'cell', [(i, i + by) for i in range(n) if 0 <= i + by < n])  27.2 us
    all_to_all x1, blocking collectives, local(): back = lax.all_to_all(ret, AXES, split_axis=0, concat_axis=0, tiled=True)  24 us
    pallas_call x1, Pallas kernels, local(): pl.pallas_call(functools.partial(pack_kernel, devices, cap), out_shape=(j...  14.3 us
    pallas_call x1, Pallas kernels, local(): pl.pallas_call(functools.partial(gather_kernel, devices, cap, block_local...  12.9 us
  transfers between devices with their start and end apart: 14, of which 7 were waited for; matrix products, arithmetic and copies ran while one was open for 2% of the time, Pallas kernels for 10%

profile of v1, /device:TPU:0, one launch (start us, length us, event | category | flops | bytes accessed | tf_op | source)
XLA Modules:
  0.0 320.2 jit_solution(3526706973893463842)
XLA Ops:
  7.2 1.6 copy.23.dir_col
  8.8 14.3 %pack.1 = (bf16[32,144,128]{2,1,0:T(8,128)(2,1)}, f32[32,128]{1,0:T(8,128)}) custom-call(s32[16,128]{1,0:T(8,128)} %bitcast.38, s32[16,128]{1,0:T(8,128)} %bitcast.39, s32[16,128]{1,0:T(8,128)} %bitcast.40, s32[16,128]{1,0:T(8,128)} %bitcast.41, f32[256,1]{1,0:T(8,128)} %copy.23.dir_col, bf16[2048,128]{1,0:T(8,128)(2,1)} %tiles.1), custom_call_target="tpu_custom_call" | custom-call | tf_op jit(solution)/shard_map/pack/pallas_call | solution.py:269
  23.1 38.0 %all_to_all.15.got = bf16[32,144,128]{2,1,0:T(8,128)(2,1)S(1)} all-to-all(bf16[32,144,128]{2,1,0:T(8,128)(2,1)} %get-tuple-element.11), channel_id=1, replica_groups=mesh['cell'=4,'tm'=8] {'cell','tm'}, dimensions={0} | all-to-all | bytes 2359296 | tf_op jit(solution)/shard_map/all_to_all | solution.py:287
  62.4 11.8 %scatter.1 = (bf16[256,1152]{1,0:T(8,128)(2,1)}, bf16[256,1152]{1,0:T(8,128)(2,1)}) custom-call(s32[4096]{0:T(1024)} %get-tuple-element.21.place, f32[4096]{0:T(1024)} %get-tuple-element.20.weight, s32[32]{0:T(128)} %convert_reduce_fusion.count, bf16[32,144,128]{2,1,0:T(8,128)(2,1)} %copy-done.2), custom_call_target="tpu_custom_call" | custom-call | tf_op jit(solution)/shard_map/scatter/pallas_call | solution.py:294
  74.9 35.1 %all-gather.5.cloned.1.call-done = bf16[2048,1152]{1,0:T(8,128)(2,1)} async-done(((bf16[256,1152]{1,0:T(8,128)(2,1)}), bf16[2048,1152]{1,0:T(8,128)(2,1)}) %all-gather.5.cloned.1.call-update) | async-done | bytes 4718608 | tf_op jit(solution)/shard_map/all_gather | solution.py:243
  110.0 3.8 %convolution_convert_fusion.refs_1_ = bf16[1152,256]{1,0:T(8,128)(2,1)S(1)} fusion(bf16[2048,1152]{1,0:T(8,128)(2,1)} %all-gather.5.cloned.1.call-done, bf16[256,2048]{1,0:T(8,128)(2,1)S(1)} %copy-done), kind=kOutput, calls=%fused_computation | convolution fusion | flops 1208254464 | bytes 6356992 | tf_op jit(solution)/shard_map/dot_general | solution.py:244
  113.8 1.3 collective-permute-start.9
  115.1 35.6 %all-gather.3.cloned.1.call-done = bf16[2048,1152]{1,0:T(8,128)(2,1)} async-done(((bf16[256,1152]{1,0:T(8,128)(2,1)}), bf16[2048,1152]{1,0:T(8,128)(2,1)}) %all-gather.3.cloned.1.call-update) | async-done | bytes 4718608 | tf_op jit(solution)/shard_map/all_gather | solution.py:243
  150.7 3.8 %convolution_convert_fusion.1.refs_0_ = bf16[1152,256]{1,0:T(8,128)(2,1)S(1)} fusion(bf16[2048,1152]{1,0:T(8,128)(2,1)} %all-gather.3.cloned.1.call-done, bf16[256,2048]{1,0:T(8,128)(2,1)S(1)} %copy-done), kind=kOutput, calls=%fused_computation.1 | convolution fusion | flops 1208254464 | bytes 6356992 | tf_op jit(solution)/shard_map/dot_general | solution.py:244
  154.5 3.4 %collective-permute-start = (bf16[1152,256]{1,0:T(8,128)(2,1)S(1)}, bf16[1152,256]{1,0:T(8,128)(2,1)S(1)}, u32[]{:S(2)}, u32[]{:S(2)}) collective-permute-start(bf16[1152,256]{1,0:T(8,128)(2,1)S(1)} %convolution_convert_fusion.1.refs_0_), channel_id=1, source_target_pairs={{0,8},{8,16},{16,24},{1,9},{9,17},{17,25},{2,10},{10,18},{18,26},{... | collective-permute-start | bytes 1769480 | tf_op jit(solution)/shard_map/ppermute | solution.py:235
  158.0 3.4 %collective-permute-start.3 = (bf16[1152,256]{1,0:T(8,128)(2,1)S(1)}, bf16[1152,256]{1,0:T(8,128)(2,1)S(1)}, u32[]{:S(2)}, u32[]{:S(2)}) collective-permute-start(bf16[1152,256]{1,0:T(8,128)(2,1)S(1)} %convolution_convert_fusion.refs_1_), channel_id=1, source_target_pairs={{0,8},{8,16},{16,24},{1,9},{9,17},{17,25},{2,10},{10,18},{18,26},{... | collective-permute-start | bytes 1769480 | tf_op jit(solution)/shard_map/ppermute | solution.py:235
  161.4 1.3 collective-permute-start.6
  162.7 1.3 collective-permute-start.10
  164.0 7.6 %collective-permute-done.refs_0_ = bf16[1152,256]{1,0:T(8,128)(2,1)S(1)} collective-permute-done((bf16[1152,256]{1,0:T(8,128)(2,1)S(1)}, bf16[1152,256]{1,0:T(8,128)(2,1)S(1)}, u32[]{:S(2)}, u32[]{:S(2)}) %collective-permute-start) | collective-permute-done | bytes 589856 | tf_op jit(solution)/shard_map/ppermute | solution.py:235
  171.6 5.2 %collective-permute-start.1 = (bf16[1152,256]{1,0:T(8,128)(2,1)S(1)}, bf16[1152,256]{1,0:T(8,128)(2,1)}, u32[]{:S(2)}, u32[]{:S(2)}) collective-permute-start(bf16[1152,256]{1,0:T(8,128)(2,1)S(1)} %collective-permute-done.refs_0_), channel_id=1, source_target_pairs={{0,8},{8,16},{16,24},{1,9},{9,17},{17,25},{2,10},{10,18},{18,26},{... | collective-permute-start | bytes 1769480 | tf_op jit(solution)/shard_map/ppermute | solution.py:235
  176.8 7.4 %collective-permute-done.3.refs_1_ = bf16[1152,256]{1,0:T(8,128)(2,1)S(1)} collective-permute-done((bf16[1152,256]{1,0:T(8,128)(2,1)S(1)}, bf16[1152,256]{1,0:T(8,128)(2,1)S(1)}, u32[]{:S(2)}, u32[]{:S(2)}) %collective-permute-start.3) | collective-permute-done | bytes 589856 | tf_op jit(solution)/shard_map/ppermute | solution.py:235
  184.3 5.3 %collective-permute-start.4 = (bf16[1152,256]{1,0:T(8,128)(2,1)S(1)}, bf16[1152,256]{1,0:T(8,128)(2,1)}, u32[]{:S(2)}, u32[]{:S(2)}) collective-permute-start(bf16[1152,256]{1,0:T(8,128)(2,1)S(1)} %collective-permute-done.3.refs_1_), channel_id=1, source_target_pairs={{0,8},{8,16},{16,24},{1,9},{9,17},{17,25},{2,10},{10,18},{18,26},{... | collective-permute-start | bytes 1769480 | tf_op jit(solution)/shard_map/ppermute | solution.py:235
  189.5 1.3 collective-permute-start.7
  190.9 1.3 collective-permute-start.11
  192.2 4.7 %collective-permute-done.1.refs_0_ = bf16[1152,256]{1,0:T(8,128)(2,1)} collective-permute-done((bf16[1152,256]{1,0:T(8,128)(2,1)S(1)}, bf16[1152,256]{1,0:T(8,128)(2,1)}, u32[]{:S(2)}, u32[]{:S(2)}) %collective-permute-start.1) | collective-permute-done | bytes 589856 | tf_op jit(solution)/shard_map/ppermute | solution.py:235
  196.9 5.3 %collective-permute-start.2 = (bf16[1152,256]{1,0:T(8,128)(2,1)}, bf16[1152,256]{1,0:T(8,128)(2,1)}, u32[]{:S(2)}, u32[]{:S(2)}) collective-permute-start(bf16[1152,256]{1,0:T(8,128)(2,1)} %collective-permute-done.1.refs_0_), channel_id=1, source_target_pairs={{0,8},{8,16},{16,24},{1,9},{9,17},{17,25},{2,10},{10,18},{18,26},{... | collective-permute-start | bytes 1769480 | tf_op jit(solution)/shard_map/ppermute | solution.py:235
  202.2 7.3 %collective-permute-done.4.refs_1_ = bf16[1152,256]{1,0:T(8,128)(2,1)} collective-permute-done((bf16[1152,256]{1,0:T(8,128)(2,1)S(1)}, bf16[1152,256]{1,0:T(8,128)(2,1)}, u32[]{:S(2)}, u32[]{:S(2)}) %collective-permute-start.4) | collective-permute-done | bytes 589856 | tf_op jit(solution)/shard_map/ppermute | solution.py:235
  209.5 5.3 %collective-permute-start.5 = (bf16[1152,256]{1,0:T(8,128)(2,1)}, bf16[1152,256]{1,0:T(8,128)(2,1)}, u32[]{:S(2)}, u32[]{:S(2)}) collective-permute-start(bf16[1152,256]{1,0:T(8,128)(2,1)} %collective-permute-done.4.refs_1_), channel_id=1, source_target_pairs={{0,8},{8,16},{16,24},{1,9},{9,17},{17,25},{2,10},{10,18},{18,26},{... | collective-permute-start | bytes 1769480 | tf_op jit(solution)/shard_map/ppermute | solution.py:235
  214.9 1.3 collective-permute-start.8
  216.2 8.8 %product.4.refs_5_ = f32[2304,256]{1,0:T(8,128)} custom-call(s32[1]{0:T(128)} %bitcast.6.here, bf16[1152,256]{1,0:T(8,128)(2,1)} %copy-done.5, bf16[1152,256]{1,0:T(8,128)(2,1)} %copy-done.3, bf16[2304,9216]{1,0:T(8,128)(2,1)} %refs_4_.5), custom_call_target="tpu_custom_call" | custom-call | flops 2717908992 | bytes 10616832 | tf_op jit(solution)/shard_map/product/pallas_call | solution.py:218
  225.0 11.9 %product.5.refs_5_ = f32[2304,256]{1,0:T(8,128)} custom-call(s32[1]{0:T(128)} %bitcast.6.here, bf16[1152,256]{1,0:T(8,128)(2,1)} %copy-done.6, bf16[1152,256]{1,0:T(8,128)(2,1)} %copy-done.7, bf16[1152,256]{1,0:T(8,128)(2,1)} %collective-permute-done.6.refs_2_, bf16[1152,256]{1,0:T(8,128)(2,1)} %copy-done.4, bf16[2304,9216]{1,0:T(8,128)(2,1)} %refs_4_.5, ...), custom_call_target="tpu_custom_call" | custom-call | flops 2717908992 | bytes 10616832 | tf_op jit(solution)/shard_map/product/pallas_call | solution.py:218
  236.9 11.9 %product.6.refs_5_ = f32[2304,256]{1,0:T(8,128)} custom-call(s32[1]{0:T(128)} %bitcast.6.here, bf16[1152,256]{1,0:T(8,128)(2,1)} %collective-permute-done.1.refs_0_, bf16[1152,256]{1,0:T(8,128)(2,1)} %collective-permute-done.4.refs_1_, bf16[1152,256]{1,0:T(8,128)(2,1)} %collective-permute-done.7.refs_2_, bf16[1152,256]{1,0:T(8,128)(2,1)} %collective-permute-done.10.refs_3_, ...), custom_call_target="tpu_custom_call" | custom-call | flops 2717908992 | bytes 10616832 | tf_op jit(solution)/shard_map/product/pallas_call | solution.py:218
  248.8 12.0 %product.7.smoothed = f32[2304,256]{1,0:T(8,128)} custom-call(s32[1]{0:T(128)} %bitcast.6.here, bf16[1152,256]{1,0:T(8,128)(2,1)} %collective-permute-done.2.refs_0_, bf16[1152,256]{1,0:T(8,128)(2,1)} %collective-permute-done.5.refs_1_, bf16[1152,256]{1,0:T(8,128)(2,1)} %collective-permute-done.8.refs_2_, bf16[1152,256]{1,0:T(8,128)(2,1)} %collective-permute-done.11.refs_3_, ...), custom_call_target="tpu_custom_call" | custom-call | flops 2717908992 | bytes 10616832 | tf_op jit(solution)/shard_map/product/pallas_call | solution.py:218
  260.7 12.9 %gather.1 = f32[32,2,128]{2,1,0:T(2,128)} custom-call(s32[4096]{0:T(1024)} %get-tuple-element.21.place, s32[32]{0:T(128)} %convert_reduce_fusion.count, bf16[32,144,128]{2,1,0:T(8,128)(2,1)} %copy-done.2, f32[2304,256]{1,0:T(8,128)} %product.7.smoothed, f32[32,128]{1,0:T(8,128)} %get-tuple-element.19.dirs, f32[2,128]{1,0:T(2,128)} %bitcast.42, ...), custom_call_target="tpu_custom_call" | custom-call | tf_op jit(solution)/shard_map/gather/pallas_call | solution.py:305
  273.6 24.0 %all_to_all.16 = f32[32,2,128]{2,1,0:T(2,128)S(1)} all-to-all(f32[32,2,128]{2,1,0:T(2,128)} %gather.1), channel_id=1, replica_groups=mesh['cell'=4,'tm'=8] {'cell','tm'}, dimensions={0} | all-to-all | bytes 65536 | tf_op jit(solution)/shard_map/all_to_all | solution.py:313
  298.3 2.1 finish.1
  300.4 9.7 %all_to_all.17 = f32[32,1,128]{2,1,0:T(1,128)S(1)} all-to-all(f32[32,1,128]{2,1,0:T(1,128)} %get-tuple-element.17), channel_id=1, replica_groups=mesh['cell'=4,'tm'=8] {'cell','tm'}, dimensions={0} | all-to-all | bytes 32768 | tf_op jit(solution)/shard_map/all_to_all | solution.py:326
  (37 shorter events, 4.8 us)
Async XLA Ops:
  7.2 102.9 %copy-start = (bf16[256,2048]{1,0:T(8,128)(2,1)S(1)}, bf16[256,2048]{1,0:T(8,128)(2,1)}, u32[]{:S(2)}) copy-start(bf16[256,2048]{1,0:T(8,128)(2,1)} %param.21) | copy-start | bytes 3145732
  7.2 102.9 %all-gather.5.cloned.1.call-start = ((), (), s32[]{:S(2)}) async-start(), calls=%async_computation.4 | async-start | bytes 5308416 | tf_op jit(solution)/shard_map/all_gather | solution.py:243
  61.0 1.4 copy-start.2
  74.2 76.6 %all-gather.3.cloned.1.call-start = ((), (), s32[]{:S(2)}) async-start(), calls=%async_computation.3 | async-start | bytes 5308416 | tf_op jit(solution)/shard_map/all_gather | solution.py:243
  113.8 102.3 %copy-start.3 = (bf16[1152,256]{1,0:T(8,128)(2,1)}, bf16[1152,256]{1,0:T(8,128)(2,1)S(1)}, u32[]{:S(2)}) copy-start(bf16[1152,256]{1,0:T(8,128)(2,1)S(1)} %convolution_convert_fusion.refs_1_) | copy-start | bytes 1769476
  113.8 48.8 %collective-permute-start.9 = (bf16[1152,256]{1,0:T(8,128)(2,1)S(1)}, bf16[1152,256]{1,0:T(8,128)(2,1)S(1)}, u32[]{:S(2)}, u32[]{:S(2)}) collective-permute-start(bf16[1152,256]{1,0:T(8,128)(2,1)S(1)} %convolution_convert_fusion.refs_1_), channel_id=1, source_target_pairs={{8,0},{16,8},{24,16},{9,1},{17,9},{25,17},{10,2},{18,10},{26,18},{... | collective-permute-start | bytes 1769480 | tf_op jit(solution)/shard_map/ppermute | solution.py:235
  154.5 61.6 %copy-start.5 = (bf16[1152,256]{1,0:T(8,128)(2,1)}, bf16[1152,256]{1,0:T(8,128)(2,1)S(1)}, u32[]{:S(2)}) copy-start(bf16[1152,256]{1,0:T(8,128)(2,1)S(1)} %convolution_convert_fusion.1.refs_0_) | copy-start | bytes 1769476
  154.5 17.1 %collective-permute-start = (bf16[1152,256]{1,0:T(8,128)(2,1)S(1)}, bf16[1152,256]{1,0:T(8,128)(2,1)S(1)}, u32[]{:S(2)}, u32[]{:S(2)}) collective-permute-start(bf16[1152,256]{1,0:T(8,128)(2,1)S(1)} %convolution_convert_fusion.1.refs_0_), channel_id=1, source_target_pairs={{0,8},{8,16},{16,24},{1,9},{9,17},{17,25},{2,10},{10,18},{18,26},{... | collective-permute-start | bytes 1769480 | tf_op jit(solution)/shard_map/ppermute | solution.py:235
  158.0 26.3 %collective-permute-start.3 = (bf16[1152,256]{1,0:T(8,128)(2,1)S(1)}, bf16[1152,256]{1,0:T(8,128)(2,1)S(1)}, u32[]{:S(2)}, u32[]{:S(2)}) collective-permute-start(bf16[1152,256]{1,0:T(8,128)(2,1)S(1)} %convolution_convert_fusion.refs_1_), channel_id=1, source_target_pairs={{0,8},{8,16},{16,24},{1,9},{9,17},{17,25},{2,10},{10,18},{18,26},{... | collective-permute-start | bytes 1769480 | tf_op jit(solution)/shard_map/ppermute | solution.py:235
  161.4 28.2 %collective-permute-start.6 = (bf16[1152,256]{1,0:T(8,128)(2,1)S(1)}, bf16[1152,256]{1,0:T(8,128)(2,1)}, u32[]{:S(2)}, u32[]{:S(2)}) collective-permute-start(bf16[1152,256]{1,0:T(8,128)(2,1)S(1)} %convolution_convert_fusion.1.refs_0_), channel_id=1, source_target_pairs={{8,0},{16,8},{24,16},{9,1},{17,9},{25,17},{10,2},{18,10},{26,18},{... | collective-permute-start | bytes 1769480 | tf_op jit(solution)/shard_map/ppermute | solution.py:235
  162.7 62.3 %copy-start.4 = (bf16[1152,256]{1,0:T(8,128)(2,1)}, bf16[1152,256]{1,0:T(8,128)(2,1)S(1)}, u32[]{:S(2)}) copy-start(bf16[1152,256]{1,0:T(8,128)(2,1)S(1)} %collective-permute-done.9.refs_3_) | copy-start | bytes 1769476
  162.7 28.2 %collective-permute-start.10 = (bf16[1152,256]{1,0:T(8,128)(2,1)S(1)}, bf16[1152,256]{1,0:T(8,128)(2,1)}, u32[]{:S(2)}, u32[]{:S(2)}) collective-permute-start(bf16[1152,256]{1,0:T(8,128)(2,1)S(1)} %collective-permute-done.9.refs_3_), channel_id=1, source_target_pairs={{8,0},{16,8},{24,16},{9,1},{17,9},{25,17},{10,2},{18,10},{26,18},{... | collective-permute-start | bytes 1769480 | tf_op jit(solution)/shard_map/ppermute | solution.py:235
  171.6 53.3 %copy-start.6 = (bf16[1152,256]{1,0:T(8,128)(2,1)}, bf16[1152,256]{1,0:T(8,128)(2,1)S(1)}, u32[]{:S(2)}) copy-start(bf16[1152,256]{1,0:T(8,128)(2,1)S(1)} %collective-permute-done.refs_0_) | copy-start | bytes 1769476
  171.6 25.3 %collective-permute-start.1 = (bf16[1152,256]{1,0:T(8,128)(2,1)S(1)}, bf16[1152,256]{1,0:T(8,128)(2,1)}, u32[]{:S(2)}, u32[]{:S(2)}) collective-permute-start(bf16[1152,256]{1,0:T(8,128)(2,1)S(1)} %collective-permute-done.refs_0_), channel_id=1, source_target_pairs={{0,8},{8,16},{16,24},{1,9},{9,17},{17,25},{2,10},{10,18},{18,26},{... | collective-permute-start | bytes 1769480 | tf_op jit(solution)/shard_map/ppermute | solution.py:235
  184.3 40.7 %copy-start.7 = (bf16[1152,256]{1,0:T(8,128)(2,1)}, bf16[1152,256]{1,0:T(8,128)(2,1)S(1)}, u32[]{:S(2)}) copy-start(bf16[1152,256]{1,0:T(8,128)(2,1)S(1)} %collective-permute-done.3.refs_1_) | copy-start | bytes 1769476
  184.3 25.3 %collective-permute-start.4 = (bf16[1152,256]{1,0:T(8,128)(2,1)S(1)}, bf16[1152,256]{1,0:T(8,128)(2,1)}, u32[]{:S(2)}, u32[]{:S(2)}) collective-permute-start(bf16[1152,256]{1,0:T(8,128)(2,1)S(1)} %collective-permute-done.3.refs_1_), channel_id=1, source_target_pairs={{0,8},{8,16},{16,24},{1,9},{9,17},{17,25},{2,10},{10,18},{18,26},{... | collective-permute-start | bytes 1769480 | tf_op jit(solution)/shard_map/ppermute | solution.py:235
  189.5 25.3 %collective-permute-start.7 = (bf16[1152,256]{1,0:T(8,128)(2,1)}, bf16[1152,256]{1,0:T(8,128)(2,1)}, u32[]{:S(2)}, u32[]{:S(2)}) collective-permute-start(bf16[1152,256]{1,0:T(8,128)(2,1)} %collective-permute-done.6.refs_2_), channel_id=1, source_target_pairs={{8,0},{16,8},{24,16},{9,1},{17,9},{25,17},{10,2},{18,10},{26,18},{... | collective-permute-start | bytes 1769480 | tf_op jit(solution)/shard_map/ppermute | solution.py:235
  190.9 57.8 %collective-permute-start.11 = (bf16[1152,256]{1,0:T(8,128)(2,1)}, bf16[1152,256]{1,0:T(8,128)(2,1)}, u32[]{:S(2)}, u32[]{:S(2)}) collective-permute-start(bf16[1152,256]{1,0:T(8,128)(2,1)} %collective-permute-done.10.refs_3_), channel_id=1, source_target_pairs={{8,0},{16,8},{24,16},{9,1},{17,9},{25,17},{10,2},{18,10},{26,18},{... | collective-permute-start | bytes 1769480 | tf_op jit(solution)/shard_map/ppermute | solution.py:235
  196.9 51.8 %collective-permute-start.2 = (bf16[1152,256]{1,0:T(8,128)(2,1)}, bf16[1152,256]{1,0:T(8,128)(2,1)}, u32[]{:S(2)}, u32[]{:S(2)}) collective-permute-start(bf16[1152,256]{1,0:T(8,128)(2,1)} %collective-permute-done.1.refs_0_), channel_id=1, source_target_pairs={{0,8},{8,16},{16,24},{1,9},{9,17},{17,25},{2,10},{10,18},{18,26},{... | collective-permute-start | bytes 1769480 | tf_op jit(solution)/shard_map/ppermute | solution.py:235
  209.5 39.2 %collective-permute-start.5 = (bf16[1152,256]{1,0:T(8,128)(2,1)}, bf16[1152,256]{1,0:T(8,128)(2,1)}, u32[]{:S(2)}, u32[]{:S(2)}) collective-permute-start(bf16[1152,256]{1,0:T(8,128)(2,1)} %collective-permute-done.4.refs_1_), channel_id=1, source_target_pairs={{0,8},{8,16},{16,24},{1,9},{9,17},{17,25},{2,10},{10,18},{18,26},{... | collective-permute-start | bytes 1769480 | tf_op jit(solution)/shard_map/ppermute | solution.py:235
  214.9 33.9 %collective-permute-start.8 = (bf16[1152,256]{1,0:T(8,128)(2,1)}, bf16[1152,256]{1,0:T(8,128)(2,1)}, u32[]{:S(2)}, u32[]{:S(2)}) collective-permute-start(bf16[1152,256]{1,0:T(8,128)(2,1)} %collective-permute-done.7.refs_2_), channel_id=1, source_target_pairs={{8,0},{16,8},{24,16},{9,1},{17,9},{25,17},{10,2},{18,10},{26,18},{... | collective-permute-start | bytes 1769480 | tf_op jit(solution)/shard_map/ppermute | solution.py:235
  248.7 63.3 %copy-start.8 = (f32[256]{0:T(256)S(1)}, f32[256]{0:T(256)}, u32[]{:S(2)}) copy-start(f32[256]{0:T(256)} %param.13) | copy-start | bytes 3076
  248.8 64.6 %copy-start.1 = (bf16[256,2048]{1,0:T(8,128)(2,1)S(1)}, bf16[256,2048]{1,0:T(8,128)(2,1)}, u32[]{:S(2)}) copy-start(bf16[256,2048]{1,0:T(8,128)(2,1)} %param.21) | copy-start | bytes 3145732
Sparse Core Ops, SparseCore 0:
  74.3 35.6 all-gather.4
  111.9 38.7 all-gather.2
